TPU v7x, 32 devices: a whole 2x2x4 slice. The times are simulated.
32 devices in a mesh: stage: 2 (over x), model: 4 (over z), data: 4 (over y, core).
Axes of the slice: x: 2, y: 2, z: 4, core: 2. Of those that a mesh axis runs over, the one named last changes fastest.
Arguments:
- w_fc1: float32 [32, 1536, 1024], P('stage', 'data', 'model'), parts along dimension 0
- m_fc1: float32 [32, 1536, 1024], P('stage', 'data', 'model'), parts along dimension 0
- g_fc1: bfloat16 [32, 1536, 1024], P('stage', 'data', 'model'), parts along dimension 0
- w_fc2: float32 [32, 1536, 512], P('stage', 'data', 'model'), parts along dimension 0
- m_fc2: float32 [32, 1536, 512], P('stage', 'data', 'model'), parts along dimension 0
- g_fc2: bfloat16 [32, 1536, 512], P('stage', 'data', 'model'), parts along dimension 0
Outputs:
- output 1: float32 [32, 1536, 1024], P('stage', 'data', 'model'), parts along dimension 0
- output 2: float32 [32, 1536, 1024], P('stage', 'data', 'model'), parts along dimension 0
- output 3: float32 [32, 1536, 512], P('stage', 'data', 'model'), parts along dimension 0
- output 4: float32 [32, 1536, 512], P('stage', 'data', 'model'), parts along dimension 0
There are 2 independent parts. A program takes and returns all parts, laid end to end along the dimension named above; each array names one.
All inputs are finite; a program needn't handle non-finite values.
Results may differ from a plain program's by a relative error of at most 0.0082908.
Values are sent between devices in bfloat16 or wider.
A program may use at most 1 GiB of HBM per device.

v0:
```python
import math
import jax
import jax.numpy as jnp
from jax import lax
from jax.sharding import PartitionSpec as P

NS_STEPS = 5
NS_COEF_A = 3.4445
NS_COEF_B = -4.7750
NS_COEF_C = 2.0315
MOMENTUM = 0.95
LEARN_RATE = 0.04
DECAY = 0.2
NORM_EPS = 1e-7


def newton_schulz(x_mat):
    row_count, col_count = x_mat.shape[1], x_mat.shape[2]
    for ns_step in range(NS_STEPS):
        if row_count <= col_count:
            gram_mat = jnp.einsum('emk,enk->emn', x_mat, x_mat, preferred_element_type=jnp.float32).astype(jnp.bfloat16)
        else:
            gram_mat = jnp.einsum('ekm,ekn->emn', x_mat, x_mat, preferred_element_type=jnp.float32).astype(jnp.bfloat16)
        gram_sq = jnp.einsum('emk,ekn->emn', gram_mat, gram_mat, preferred_element_type=jnp.float32)
        poly_mat = (NS_COEF_B * gram_mat.astype(jnp.float32) + NS_COEF_C * gram_sq).astype(jnp.bfloat16)
        if row_count <= col_count:
            update_term = jnp.einsum('emk,ekn->emn', poly_mat, x_mat, preferred_element_type=jnp.float32)
        else:
            update_term = jnp.einsum('emk,ekn->emn', x_mat, poly_mat, preferred_element_type=jnp.float32)
        x_mat = (NS_COEF_A * x_mat.astype(jnp.float32) + update_term).astype(jnp.bfloat16)
    return x_mat


def update_stack(w_loc, m_loc, g_loc, data_size, model_size):
    new_mom = MOMENTUM * m_loc + g_loc.astype(jnp.float32)
    mat_norms = jnp.sqrt(lax.psum(jnp.sum(new_mom * new_mom, axis=(1, 2)), ('data', 'model')))
    expert_count, rows_loc, cols_loc = m_loc.shape
    own_count = expert_count // data_size
    rows_full = rows_loc * data_size
    cols_full = cols_loc * model_size
    row_whole = lax.all_to_all(new_mom.astype(jnp.bfloat16), 'data', 0, 1, tiled=True)
    mom_whole = lax.all_gather(row_whole, 'model', axis=2, tiled=True)
    own_norms = lax.dynamic_slice_in_dim(mat_norms, lax.axis_index('data') * own_count, own_count)
    x_mat = (mom_whole.astype(jnp.float32) / (own_norms[:, None, None] + NORM_EPS)).astype(jnp.bfloat16)
    x_mat = newton_schulz(x_mat)
    x_cols = lax.dynamic_slice_in_dim(x_mat, lax.axis_index('model') * cols_loc, cols_loc, axis=2)
    x_back = lax.all_to_all(x_cols, 'data', 1, 0, tiled=True)
    step_scale = 0.2 * math.sqrt(max(rows_full, cols_full))
    new_w = w_loc - LEARN_RATE * (x_back.astype(jnp.float32) * step_scale + DECAY * w_loc)
    return new_w, new_mom


def solution(mesh):
    data_size = mesh.shape['data']
    model_size = mesh.shape['model']
    block_spec = P('stage', 'data', 'model')

    def local_step(w_fc1, m_fc1, g_fc1, w_fc2, m_fc2, g_fc2):
        new_w1, new_m1 = update_stack(w_fc1, m_fc1, g_fc1, data_size, model_size)
        new_w2, new_m2 = update_stack(w_fc2, m_fc2, g_fc2, data_size, model_size)
        return new_w1, new_m1, new_w2, new_m2

    return jax.shard_map(local_step, mesh=mesh, in_specs=(block_spec,) * 6, out_specs=(block_spec,) * 4, check_vma=False)
```

profile of v0, /device:TPU:0, one launch (start us, length us, event | category | flops | bytes accessed | tf_op | source)
XLA Modules:
  0.0 740.5 jit_solution(2882478140170269807)
XLA Ops:
  7.2 2.9 fusion.39
  10.2 24.1 %all_to_all.54 = bf16[16,384,128]{2,1,0:T(8,128)(2,1)S(1)} all-to-all(bf16[16,384,128]{2,1,0:T(8,128)(2,1)S(1)} %get-tuple-element.6), channel_id=1, replica_groups=mesh['stage'=2,'model'=4,'data'=4] {'data'}, dimensions={0} | all-to-all | bytes 3145728 | tf_op jit(solution)/shard_map/all_to_all | solution.py:41
  35.6 4.9 multiply_reduce_fusion
  40.9 39.4 %all_to_all.55 = bf16[16,384,256]{2,1,0:T(8,128)(2,1)S(1)} all-to-all(bf16[16,384,256]{2,1,0:T(8,128)(2,1)S(1)} %convert_element_type.187), channel_id=1, replica_groups=mesh['stage'=2,'model'=4,'data'=4] {'data'}, dimensions={0} | all-to-all | bytes 6291456 | tf_op jit(solution)/shard_map/all_to_all | solution.py:41
  80.4 2.0 copy.24
  82.7 42.8 %all-reduce = (f32[16]{0:T(128)S(1)}, f32[16]{0:T(128)S(1)}) all-reduce(f32[16]{0:T(128)S(1)} %get-tuple-element.8, f32[16]{0:T(128)S(1)} %multiply_reduce_fusion.1), channel_id=1, replica_groups=mesh['stage'=2,'model'=4,'data'=4] {'data','model'}, use_global_device_ids=true, to_apply=%region_1.0 | all-reduce | flops 32 | bytes 256 | tf_op jit(solution)/shard_map/psum | solution.py:36
  125.7 27.5 %all-gather.5.cloned.1.call-done = bf16[4,1536,512]{2,1,0:T(8,128)(2,1)} async-done(((bf16[4,1536,128]{2,1,0:T(8,128)(2,1)}), bf16[4,1536,512]{2,1,0:T(8,128)(2,1)}) %all-gather.5.cloned.1.call-update) | async-done | bytes 6291472 | tf_op jit(solution)/shard_map/all_gather | solution.py:42
  153.2 8.6 %fusion.37 = bf16[4,512,512]{2,1,0:T(8,128)(2,1)S(1)} fusion(bf16[4,1536,512]{2,1,0:T(8,128)(2,1)} %all-gather.5.cloned.1.call-done, f32[4]{0:T(128)S(1)} %dynamic-slice_add_fusion.2), kind=kOutput, calls=%fused_computation.59 | convolution fusion | flops 3230662656 | bytes 8388624 | tf_op jit(solution)/shard_map/ekm,ekn->emn/dot_general | solution.py:23
  161.8 1.3 add_convert_fusion.17
  163.1 1.5 copy-done.4
  164.6 4.1 add_convert_fusion.12
  168.7 3.7 fusion.45
  172.5 1.3 add_convert_fusion.16
  173.8 5.4 add_convert_fusion.11
  179.3 8.1 %fusion.46 = bf16[4,512,512]{2,1,0:T(8,128)(2,1)S(1)} fusion(bf16[4,1536,512]{2,1,0:T(8,128)(2,1)} %add_convert_fusion.11), kind=kOutput, calls=%fused_computation.68 | convolution fusion | flops 3221225472 | bytes 8388608 | tf_op jit(solution)/shard_map/ekm,ekn->emn/dot_general | solution.py:23
  187.4 1.3 add_convert_fusion.15
  188.8 1.4 copy-done.5
  190.2 5.3 add_convert_fusion.10
  195.5 8.1 %fusion.47 = bf16[4,512,512]{2,1,0:T(8,128)(2,1)S(1)} fusion(bf16[4,1536,512]{2,1,0:T(8,128)(2,1)} %add_convert_fusion.10), kind=kOutput, calls=%fused_computation.69 | convolution fusion | flops 3221225472 | bytes 8388608 | tf_op jit(solution)/shard_map/ekm,ekn->emn/dot_general | solution.py:23
  203.6 1.3 add_convert_fusion.14
  204.9 7.6 %add_convert_fusion.9 = bf16[4,1536,512]{2,1,0:T(8,128)(2,1)S(1)} fusion(bf16[4,1536,512]{2,1,0:T(8,128)(2,1)} %add_convert_fusion.10, bf16[4,512,512]{2,1,0:T(8,128)(2,1)S(1)} %add_convert_fusion.14), kind=kOutput, calls=%fused_computation.10 | convolution fusion | flops 3233808384 | bytes 14680064 | tf_op jit(solution)/shard_map/emk,ekn->emn/dot_general | solution.py:29
  212.5 2.7 copy-done.3
  215.2 3.9 fusion.48
  219.1 9.4 %fusion.25 = f32[4,1536,512]{2,1,0:T(8,128)} fusion(bf16[4,1536,512]{2,1,0:T(8,128)(2,1)} %copy-done.3, bf16[4,512,512]{2,1,0:T(8,128)(2,1)S(1)} %fusion.48), kind=kOutput, calls=%fused_computation.46 | convolution fusion | flops 4300210176 | bytes 20971520 | tf_op jit(solution)/shard_map/emk,ekn->emn/dot_general | solution.py:29
  228.6 2.8 fusion.8
  231.4 8.2 %copy.38 = bf16[4,1536,128]{2,0,1:T(4,128)(2,1)} copy(bf16[4,1536,128]{2,1,0:T(8,128)(2,1)S(1)} %fusion.8) | data formatting | bytes 3145728 | tf_op jit(solution)/shard_map/dynamic_slice | solution.py:46
  239.6 4.8 all-to-all-start.3
  244.3 127.8 %all-gather.3.cloned.1.call-done = bf16[4,1536,1024]{2,1,0:T(8,128)(2,1)} async-done(((bf16[4,1536,256]{2,1,0:T(8,128)(2,1)}), bf16[4,1536,1024]{2,1,0:T(8,128)(2,1)}) %all-gather.3.cloned.1.call-update) | async-done | bytes 12582928 | tf_op jit(solution)/shard_map/all_gather | solution.py:42
  372.1 25.1 %fusion.38 = bf16[4,1024,1024]{2,1,0:T(8,128)(2,1)} fusion(bf16[4,1536,1024]{2,1,0:T(8,128)(2,1)} %all-gather.3.cloned.1.call-done, f32[4]{0:T(128)S(1)} %dynamic-slice_add_fusion.3), kind=kOutput, calls=%fused_computation.60 | convolution fusion | flops 12903776256 | bytes 20971536 | tf_op jit(solution)/shard_map/ekm,ekn->emn/dot_general | solution.py:23
  397.2 17.7 %add_convert_fusion.8.clone.5 = bf16[4,1024,1024]{2,1,0:T(8,128)(2,1)} fusion(bf16[4,1024,1024]{2,1,0:T(8,128)(2,1)} %fusion.38), kind=kOutput, calls=%fused_computation.9.clone.clone.clone.2 | convolution fusion | flops 8610906112 | bytes 16777216 | tf_op jit(solution)/shard_map/emk,ekn->emn/dot_general | solution.py:24
  414.9 22.7 %add_convert_fusion.3 = bf16[4,1536,1024]{2,1,0:T(8,128)(2,1)} fusion(f32[4]{0:T(128)S(1)} %dynamic-slice_add_fusion.3, bf16[4,1536,1024]{2,1,0:T(8,128)(2,1)} %all-gather.3.cloned.1.call-done, bf16[4,1024,1024]{2,1,0:T(8,128)(2,1)} %add_convert_fusion.8.clone.5), kind=kOutput, calls=%fused_computation.3 | convolution fusion | flops 12947816448 | bytes 33554448 | tf_op jit(solution)/shard_map/emk,ekn->emn/dot_general | solution.py:29
  437.6 21.8 %fusion.40 = bf16[4,1024,1024]{2,1,0:T(8,128)(2,1)} fusion(bf16[4,1536,1024]{2,1,0:T(8,128)(2,1)} %add_convert_fusion.3), kind=kOutput, calls=%fused_computation.62 | convolution fusion | flops 12884901888 | bytes 20971520 | tf_op jit(solution)/shard_map/ekm,ekn->emn/dot_general | solution.py:23
  459.3 33.7 %add_convert_fusion.2 = bf16[4,1536,1024]{2,1,0:T(8,128)(2,1)} fusion(bf16[4,1536,1024]{2,1,0:T(8,128)(2,1)} %add_convert_fusion.3, bf16[4,1024,1024]{2,1,0:T(8,128)(2,1)} %fusion.40), kind=kOutput, calls=%fused_computation.2 | convolution fusion | flops 21520973824 | bytes 33554432 | tf_op jit(solution)/shard_map/emk,ekn->emn/dot_general | solution.py:29
  493.0 21.8 %fusion.41 = bf16[4,1024,1024]{2,1,0:T(8,128)(2,1)} fusion(bf16[4,1536,1024]{2,1,0:T(8,128)(2,1)} %add_convert_fusion.2), kind=kOutput, calls=%fused_computation.63 | convolution fusion | flops 12884901888 | bytes 20971520 | tf_op jit(solution)/shard_map/ekm,ekn->emn/dot_general | solution.py:23
  514.8 34.1 %add_convert_fusion.1 = bf16[4,1536,1024]{2,1,0:T(8,128)(2,1)} fusion(bf16[4,1536,1024]{2,1,0:T(8,128)(2,1)} %add_convert_fusion.2, bf16[4,1024,1024]{2,1,0:T(8,128)(2,1)} %fusion.41), kind=kOutput, calls=%fused_computation.1 | convolution fusion | flops 21520973824 | bytes 33554432 | tf_op jit(solution)/shard_map/emk,ekn->emn/dot_general | solution.py:29
  548.8 21.8 %fusion.42 = bf16[4,1024,1024]{2,1,0:T(8,128)(2,1)} fusion(bf16[4,1536,1024]{2,1,0:T(8,128)(2,1)} %add_convert_fusion.1), kind=kOutput, calls=%fused_computation.64 | convolution fusion | flops 12884901888 | bytes 20971520 | tf_op jit(solution)/shard_map/ekm,ekn->emn/dot_general | solution.py:23
  570.6 34.1 %add_convert_fusion = bf16[4,1536,1024]{2,1,0:T(8,128)(2,1)} fusion(bf16[4,1536,1024]{2,1,0:T(8,128)(2,1)} %add_convert_fusion.1, bf16[4,1024,1024]{2,1,0:T(8,128)(2,1)} %fusion.42), kind=kOutput, calls=%fused_computation | convolution fusion | flops 21520973824 | bytes 33554432 | tf_op jit(solution)/shard_map/emk,ekn->emn/dot_general | solution.py:29
  604.8 21.8 %fusion.43 = bf16[4,1024,1024]{2,1,0:T(8,128)(2,1)} fusion(bf16[4,1536,1024]{2,1,0:T(8,128)(2,1)} %add_convert_fusion), kind=kOutput, calls=%fused_computation.65 | convolution fusion | flops 12884901888 | bytes 20971520 | tf_op jit(solution)/shard_map/ekm,ekn->emn/dot_general | solution.py:23
  626.6 17.6 %add_convert_fusion.4 = bf16[4,1024,1024]{2,1,0:T(8,128)(2,1)} fusion(bf16[4,1024,1024]{2,1,0:T(8,128)(2,1)} %fusion.43), kind=kOutput, calls=%fused_computation.5 | convolution fusion | flops 8610906112 | bytes 16777216 | tf_op jit(solution)/shard_map/emk,ekn->emn/dot_general | solution.py:24
  644.2 23.1 %fusion.44 = f32[4,1536,1024]{2,1,0:T(8,128)} fusion(bf16[4,1536,1024]{2,1,0:T(8,128)(2,1)} %add_convert_fusion, bf16[4,1024,1024]{2,1,0:T(8,128)(2,1)} %add_convert_fusion.4), kind=kOutput, calls=%fused_computation.66 | convolution fusion | flops 12884901888 | bytes 46137344 | tf_op jit(solution)/shard_map/emk,ekn->emn/dot_general | solution.py:29
  667.3 4.6 fusion.5
  671.8 13.3 %copy.30 = bf16[4,1536,256]{2,0,1:T(4,128)(2,1)} copy(bf16[4,1536,256]{2,1,0:T(8,128)(2,1)S(1)} %fusion.5) | data formatting | bytes 6291456 | tf_op jit(solution)/shard_map/dynamic_slice | solution.py:46
  685.2 3.7 all-to-all-start.1
  688.9 2.1 convert_multiply_fusion.1
  691.5 2.2 fusion.10
  693.7 31.9 %all-to-all-done.1 = bf16[4,1536,256]{2,0,1:T(4,128)(2,1)S(1)} async-done(((bf16[4,1536,256]{2,0,1:T(4,128)(2,1)}), bf16[4,1536,256]{2,0,1:T(4,128)(2,1)S(1)}, u32[]{:S(2)}, u32[]{:S(2)}) %all-to-all-start.1) | async-done | bytes 3145760 | tf_op jit(solution)/shard_map/all_to_all | solution.py:47
  725.6 1.7 convert_multiply_fusion
  729.0 4.5 fusion.7
  (28 shorter events, 4.4 us)
Async XLA Ops:
  7.2 146.0 %all-gather.5.cloned.1.call-start = ((), (), s32[]{:S(2)}) async-start(), calls=%async_computation.5 | async-start | bytes 7864320 | tf_op jit(solution)/shard_map/all_gather | solution.py:42
  10.1 72.2 %copy-start.1 = (f32[16,384,128]{2,1,0:T(8,128)}, f32[16,384,128]{2,1,0:T(8,128)S(1)}, u32[]{:S(2)}) copy-start(f32[16,384,128]{2,1,0:T(8,128)S(1)} %get-tuple-element.7) | copy-start | bytes 9437188
  35.6 336.5 %all-gather.3.cloned.1.call-start = ((), (), s32[]{:S(2)}) async-start(), calls=%async_computation.4 | async-start | bytes 15728640 | tf_op jit(solution)/shard_map/all_gather | solution.py:42
  40.5 39.8 %copy-start = (f32[16,384,256]{2,1,0:T(8,128)}, f32[16,384,256]{2,1,0:T(8,128)S(1)}, u32[]{:S(2)}) copy-start(f32[16,384,256]{2,1,0:T(8,128)S(1)} %get-tuple-element.9) | copy-start | bytes 18874372
  161.8 2.8 copy-start.4
  187.4 2.8 copy-start.5
  212.5 2.7 copy-start.3
  239.6 445.6 %all-to-all-start.3 = ((bf16[4,1536,128]{2,0,1:T(4,128)(2,1)}), bf16[4,1536,128]{2,0,1:T(4,128)(2,1)}, u32[]{:S(2)}, u32[]{:S(2)}) async-start(bf16[4,1536,128]{2,0,1:T(4,128)(2,1)} %copy.38), calls=%async_computation.3 | async-start | bytes 3145728 | tf_op jit(solution)/shard_map/all_to_all | solution.py:47
  685.2 40.4 %all-to-all-start.1 = ((bf16[4,1536,256]{2,0,1:T(4,128)(2,1)}), bf16[4,1536,256]{2,0,1:T(4,128)(2,1)S(1)}, u32[]{:S(2)}, u32[]{:S(2)}) async-start(bf16[4,1536,256]{2,0,1:T(4,128)(2,1)} %copy.30), calls=%async_computation.1 | async-start | bytes 6291456 | tf_op jit(solution)/shard_map/all_to_all | solution.py:47
  688.9 2.5 copy-start.2
  725.6 2.8 slice-start
  727.2 1.7 slice-start.1
Sparse Core Ops, SparseCore 0:
  35.7 117.4 all-gather.4
  155.3 216.7 all-gather.2
where the time goes:
time: 744 us; the launch traced here: 741 us
  matrix products  365 us (49%)
  waiting for transfers between devices  187 us (25%)
  blocking collectives  106 us (14%)
  local copies, waits for them, and re-layouts  32.5 us (4%)
  other arithmetic  26.6 us (4%)
  between operations  14.6 us (2%)
  starting transfers between devices  8.54 us (1%)
    dot_general x10, matrix products, newton_schulz(): jnp.einsum('emk,ekn->emn', x_mat, poly_mat, preferred_element_type=jnp.fl...  179 us
    all_gather x2, waiting for transfers between devices, update_stack(): mom_whole = lax.all_gather(row_whole, 'model', axis=2, tiled=True)  155 us
    dot_general x10, matrix products, newton_schulz(): jnp.einsum('ekm,ekn->emn', x_mat, x_mat, preferred_element_type=jnp.float32)  145 us
    all_to_all x2, blocking collectives, update_stack(): lax.all_to_all(new_mom.astype(jnp.bfloat16), 'data', 0, 1, tiled=True)  63.6 us
    psum x1, blocking collectives, update_stack(): lax.psum(jnp.sum(new_mom * new_mom, axis=(1, 2)), ('data', 'model'))  42.8 us
    dot_general x6, matrix products, newton_schulz(): jnp.einsum('emk,ekn->emn', gram_mat, gram_mat, preferred_element_type=jnp...  40.6 us
    all_to_all x2, waiting for transfers between devices, update_stack(): x_back = lax.all_to_all(x_cols, 'data', 1, 0, tiled=True)  31.9 us
    dynamic_slice x2, local copies, waits for them, and re-layouts, update_stack(): lax.dynamic_slice_in_dim(x_mat, lax.axis_index('model') * cols_loc, cols_...  21.5 us
  transfers between devices with their start and end apart: 4, of which 3 were waited for; matrix products, arithmetic and copies ran while one was open for 55% of the time, Pallas kernels for 0%

commit v1 on v0

v1 whole, which is shorter than its diff:
```python
import functools
import math
import jax
import jax.numpy as jnp
from jax import lax
from jax.experimental import pallas as pl
from jax.experimental.pallas import tpu as pltpu
from jax.sharding import PartitionSpec as P

NS_STEPS = 5
NS_COEF_A = 3.4445
NS_COEF_B = -4.7750
NS_COEF_C = 2.0315
MOMENTUM = 0.95
LEARN_RATE = 0.04
DECAY = 0.2
NORM_EPS = 1e-7

F32 = jnp.float32
BF16 = jnp.bfloat16
MESH = pl.DeviceIdType.MESH
TILE = 256


def flip(bit, offset):
    return bit + offset - 2 * bit * offset


def xor2(value, offset):
    high = flip(lax.div(value, 2), lax.div(offset, 2))
    low = flip(lax.rem(value, 2), lax.rem(offset, 2))
    return high * 2 + low


def fold_squares(mom):
    sq = mom * mom
    rows, cols = sq.shape
    acc = jnp.sum(sq.reshape(rows // 8, 8, cols), axis=0)
    out = acc[:, :128]
    for col in range(128, cols, 128):
        out = out + acc[:, col:col + 128]
    return out


def momentum_kernel(m1_ref, g1_ref, m2_ref, g2_ref, nm1_ref, b1_ref, nm2_ref, b2_ref, sq_ref):
    for slot, (m_ref, g_ref, nm_ref, b_ref) in enumerate(
            ((m1_ref, g1_ref, nm1_ref, b1_ref), (m2_ref, g2_ref, nm2_ref, b2_ref))):
        mom = MOMENTUM * m_ref[0] + g_ref[0].astype(F32)
        nm_ref[0] = mom
        b_ref[0] = mom.astype(BF16)
        sq_ref[0, slot * 8:slot * 8 + 8, :] = fold_squares(mom)


def momentum_step(m1, g1, m2, g2):
    experts = m1.shape[0]

    def spec(arr):
        return pl.BlockSpec((1,) + arr.shape[1:], lambda e: (e, 0, 0))
    sq_shape = jax.ShapeDtypeStruct((experts, 16, 128), F32)
    outs = (jax.ShapeDtypeStruct(m1.shape, F32), jax.ShapeDtypeStruct(m1.shape, BF16),
            jax.ShapeDtypeStruct(m2.shape, F32), jax.ShapeDtypeStruct(m2.shape, BF16), sq_shape)
    return pl.pallas_call(
        momentum_kernel, out_shape=outs, grid=(experts,),
        in_specs=[spec(m1), spec(g1), spec(m2), spec(g2)],
        out_specs=tuple(spec(o) for o in outs),
        name='momentum')(m1, g1, m2, g2)


def dot_tn(lhs, rhs):
    return lax.dot_general(lhs, rhs, (((0,), (0,)), ((), ())), preferred_element_type=F32)


def gram_and_poly(x, gram, poly):
    size = gram.shape[0]
    for blk in range(size // TILE):
        lo, hi = blk * TILE, (blk + 1) * TILE
        val = dot_tn(x[:, lo:hi], x[:, :hi]).astype(BF16)
        gram[lo:hi, :hi] = val
        if blk:
            gram[:lo, lo:hi] = val[:, :lo].T
    for blk in range(size // TILE):
        lo, hi = blk * TILE, (blk + 1) * TILE
        sq = jnp.dot(gram[lo:hi, :], gram[:, :hi], preferred_element_type=F32)
        val = (NS_COEF_B * gram[lo:hi, :hi].astype(F32) + NS_COEF_C * sq).astype(BF16)
        poly[lo:hi, :hi] = val
        if blk:
            poly[:lo, lo:hi] = val[:, :lo].T


def update_rows(x, poly, rows):
    old = x[rows, :]
    term = jnp.dot(old, poly[...], preferred_element_type=F32)
    x[rows, :] = (NS_COEF_A * old.astype(F32) + term).astype(BF16)


def newton_schulz(x, gram, poly, block_rows, last_rows):
    blocks = x.shape[0] // block_rows

    def one_block(i, carry):
        update_rows(x, poly, pl.ds(pl.multiple_of(i * block_rows, block_rows), block_rows))
        return carry

    def one_step(step, carry):
        gram_and_poly(x, gram, poly)

        @pl.when(step < NS_STEPS - 1)
        def _():
            lax.fori_loop(0, blocks, one_block, 0)
        return carry
    lax.fori_loop(0, NS_STEPS, one_step, 0)
    last_rows()


def exchange_kernel(b1_ref, b2_ref, sq_ref, o1_ref, o2_ref,
                    x1, x2, gram1, poly1, gram2, poly2, sq_in,
                    in_send, in_recv, sq_send, sq_recv, out_send, out_recv):
    data = lax.axis_index('data')
    model = lax.axis_index('model')
    me = data * 4 + model
    rows = b1_ref.shape[1]
    cols1, cols2 = b1_ref.shape[2], b2_ref.shape[2]

    def peer(slot):
        return xor2(data, lax.rem(slot, 4)), xor2(model, lax.div(slot, 4))

    def each_peer(action):
        def body(slot, carry):
            action(slot, *peer(slot))
            return carry
        lax.fori_loop(1, 16, body, 0)

    def row_slice(index):
        return pl.ds(pl.multiple_of(index * rows, rows), rows)

    def col_slice(index, cols):
        return pl.ds(pl.multiple_of(index * cols, cols), cols)

    def remote(source, target, send, recv, to_data, to_model):
        return pltpu.make_async_remote_copy(
            src_ref=source, dst_ref=target, send_sem=send, recv_sem=recv,
            device_id={'data': to_data, 'model': to_model}, device_id_type=MESH)

    barrier = pltpu.get_barrier_semaphore()

    def greet(slot, to_data, to_model):
        pl.semaphore_signal(barrier, inc=1, device_id={'data': to_data, 'model': to_model}, device_id_type=MESH)
    each_peer(greet)
    pl.semaphore_wait(barrier, 15)

    arrays = ((b1_ref, x1, o1_ref, cols1), (b2_ref, x2, o2_ref, cols2))

    def copy_sq(slot, to_data, to_model):
        return remote(sq_ref.at[to_data * 4 + to_model], sq_in.at[slot], sq_send.at[slot], sq_recv.at[slot],
                      to_data, to_model)

    def copy_in(which, slot, to_data, to_model):
        src, dst, _, cols = arrays[which]
        return remote(src.at[to_data * 4 + to_model], dst.at[row_slice(data), col_slice(model, cols)],
                      in_send.at[which, slot], in_recv.at[which, slot], to_data, to_model)

    def own_in(which):
        src, dst, _, cols = arrays[which]
        return pltpu.make_async_copy(src.at[me], dst.at[row_slice(data), col_slice(model, cols)],
                                     in_recv.at[which, 0])

    def copy_out(which, slot, to_data, to_model):
        _, src, dst, cols = arrays[which]
        return remote(src.at[row_slice(to_data), col_slice(to_model, cols)], dst.at[me],
                      out_send.at[which, slot], out_recv.at[which, slot], to_data, to_model)

    def own_out(which):
        _, src, dst, cols = arrays[which]
        return pltpu.make_async_copy(src.at[row_slice(data), col_slice(model, cols)], dst.at[me],
                                     out_recv.at[which, 0])

    each_peer(lambda *at: copy_sq(*at).start())
    for which in (1, 0):
        own_in(which).start()
        each_peer(lambda *at: copy_in(which, *at).start())

    sq_in[0] = sq_ref[me]
    each_peer(lambda *at: copy_sq(*at).wait())
    total = jnp.sum(sq_in[...], axis=0)
    norm1 = jnp.sqrt(jnp.sum(total[:8], keepdims=True)) + NORM_EPS
    norm2 = jnp.sqrt(jnp.sum(total[8:], keepdims=True)) + NORM_EPS

    def receive(which, norm):
        _, x, _, cols = arrays[which]

        def scale(from_data, from_model):
            at = (row_slice(from_data), col_slice(from_model, cols))
            x[at] = (x[at].astype(F32) / norm).astype(BF16)

        def take(slot, from_data, from_model):
            copy_in(which, slot, from_data, from_model).wait_recv()
            scale(from_data, from_model)
        own_in(which).wait()
        scale(data, model)
        each_peer(take)

    receive(1, norm2)

    def finish2():
        def body(i, carry):
            update_rows(x2, poly2, row_slice(i))
            return carry
        lax.fori_loop(0, 4, body, 0)
    newton_schulz(x2, gram2, poly2, rows, finish2)

    receive(0, norm1)
    own_out(1).start()
    each_peer(lambda *at: copy_out(1, *at).start())

    def finish1():
        update_rows(x1, poly1, row_slice(data))
        own_out(0).start()
        for dz in (1, 2, 3):
            copy_out(0, dz * 4, *peer(dz * 4)).start()

        def body(dd, carry):
            update_rows(x1, poly1, row_slice(xor2(data, dd)))
            for dz in range(4):
                slot = dz * 4 + dd
                copy_out(0, slot, *peer(slot)).start()
            return carry
        lax.fori_loop(1, 4, body, 0)
    newton_schulz(x1, gram1, poly1, rows, finish1)

    for which in (1, 0):
        each_peer(lambda *at: copy_in(which, *at).wait_send())
    for which in (1, 0):
        own_out(which).wait()
        each_peer(lambda *at: copy_out(which, *at).wait())


def exchange_step(b1, b2, sq):
    rows, cols1, cols2 = b1.shape[1], b1.shape[2], b2.shape[2]
    full_rows, size1, size2 = rows * 4, cols1 * 4, cols2 * 4
    any_spec = pl.BlockSpec(memory_space=pl.ANY)
    vmem_spec = pl.BlockSpec(memory_space=pltpu.VMEM)
    return pl.pallas_call(
        exchange_kernel,
        out_shape=(jax.ShapeDtypeStruct(b1.shape, BF16), jax.ShapeDtypeStruct(b2.shape, BF16)),
        in_specs=[any_spec, any_spec, vmem_spec],
        out_specs=(any_spec, any_spec),
        scratch_shapes=[
            pltpu.VMEM((full_rows, size1), BF16), pltpu.VMEM((full_rows, size2), BF16),
            pltpu.VMEM((size1, size1), BF16), pltpu.VMEM((size1, size1), BF16),
            pltpu.VMEM((size2, size2), BF16), pltpu.VMEM((size2, size2), BF16),
            pltpu.VMEM((16, 16, 128), F32),
            pltpu.SemaphoreType.DMA((2, 16)), pltpu.SemaphoreType.DMA((2, 16)),
            pltpu.SemaphoreType.DMA((16,)), pltpu.SemaphoreType.DMA((16,)),
            pltpu.SemaphoreType.DMA((2, 16)), pltpu.SemaphoreType.DMA((2, 16)),
        ],
        compiler_params=pltpu.CompilerParams(
            collective_id=0, has_side_effects=True, vmem_limit_bytes=48 << 20),
        name='exchange')(b1, b2, sq)


def weight_step(w, ortho, row_count, col_count):
    scale = 0.2 * math.sqrt(max(row_count, col_count))
    return w - LEARN_RATE * (ortho.astype(F32) * scale + DECAY * w)


def solution(mesh):
    data_size = mesh.shape['data']
    model_size = mesh.shape['model']
    block_spec = P('stage', 'data', 'model')

    def local_step(w1, m1, g1, w2, m2, g2):
        new_m1, b1, new_m2, b2, sq = momentum_step(m1, g1, m2, g2)
        x1, x2 = exchange_step(b1, b2, sq)
        rows = m1.shape[1] * data_size
        new_w1 = weight_step(w1, x1, rows, m1.shape[2] * model_size)
        new_w2 = weight_step(w2, x2, rows, m2.shape[2] * model_size)
        return new_w1, new_m1, new_w2, new_m2

    return jax.shard_map(local_step, mesh=mesh, in_specs=(block_spec,) * 6, out_specs=(block_spec,) * 4, check_vma=False)
```

time: 744 us -> 247 us (0.33)
  matrix products: 365 us -> 0 us
  Pallas kernels: 0 us -> 232 us
  waiting for transfers between devices: 187 us -> 0 us
  blocking collectives: 106 us -> 0 us
  local copies, waits for them, and re-layouts: 32.5 us -> 2.32 us
  other arithmetic: 26.6 us -> 10.1 us
  between operations: 14.6 us -> 0.65 us
  starting transfers between devices: 8.54 us -> 0 us
    dot_general x26 -> x0, matrix products: 365 us -> none  [the longest x10 179 us: newton_schulz(): jnp.einsum('emk,ekn->emn', x_mat, poly_mat, preferred_element_type=jnp.fl...]
    pallas_call x0 -> x2, Pallas kernels: none -> 232 us  [the longest x1 216 us: exchange_step(): pl.pallas_call(exchange_kernel, out_shape=(jax.ShapeDtypeStruct(b1.shape,...]
    all_gather x2 -> x0, waiting for transfers between devices: 155 us -> none  [update_stack(): mom_whole = lax.all_gather(row_whole, 'model', axis=2, tiled=True)]
    all_to_all x2 -> x0, blocking collectives: 63.6 us -> none  [update_stack(): lax.all_to_all(new_mom.astype(jnp.bfloat16), 'data', 0, 1, tiled=True)]
    psum x1 -> x0, blocking collectives: 42.8 us -> none  [update_stack(): lax.psum(jnp.sum(new_mom * new_mom, axis=(1, 2)), ('data', 'model'))]
    all_to_all x2 -> x0, waiting for transfers between devices: 31.9 us -> none  [update_stack(): x_back = lax.all_to_all(x_cols, 'data', 1, 0, tiled=True)]
    dynamic_slice x2 -> x0, local copies, waits for them, and re-layouts: 21.5 us -> none  [update_stack(): lax.dynamic_slice_in_dim(x_mat, lax.axis_index('model') * cols_loc, cols_...]
    convert_element_type x4 -> x0, other arithmetic: 10.7 us -> none  [the longest x2 7.37 us: newton_schulz(): (NS_COEF_A * x_mat.astype(jnp.float32) + update_term).astype(jnp.bfloat16)]
  transfers between devices with their start and end apart: 4 -> 0, of which waited for: 3 -> 0; matrix products, arithmetic and copies ran while one was open for 55% -> 0% of each run, Pallas kernels for 0% -> 0%
where the time goes in v1:
time: 247 us; the launch traced here: 245 us
  Pallas kernels  232 us (94%)
  other arithmetic  10.1 us (4%)
    pallas_call x1, Pallas kernels, exchange_step(): pl.pallas_call(exchange_kernel, out_shape=(jax.ShapeDtypeStruct(b1.shape,...  216 us
    pallas_call x1, Pallas kernels, momentum_step(): pl.pallas_call(momentum_kernel, out_shape=outs, grid=(experts,), in_specs...  15.8 us
    sub x2, other arithmetic, weight_step(): return w - LEARN_RATE * (ortho.astype(F32) * scale + DECAY * w)  10.1 us

profile of v1, /device:TPU:0, one launch (start us, length us, event | category | flops | bytes accessed | tf_op | source)
XLA Modules:
  0.0 245.3 jit_solution(12517728028975159174)
XLA Ops:
  0.6 15.8 %momentum.1 = (f32[16,384,256]{2,1,0:T(8,128)}, bf16[16,384,256]{2,1,0:T(8,128)(2,1)}, f32[16,384,128]{2,1,0:T(8,128)}, bf16[16,384,128]{2,1,0:T(8,128)(2,1)}, f32[16,16,128]{2,1,0:T(8,128)}) custom-call(f32[16,384,256]{2,1,0:T(8,128)} %m1_ref.1, bf16[16,384,256]{2,1,0:T(8,128)(2,1)} %g1_ref.1, f32[16,384,128]{2,1,0:T(8,128)} %m2_ref.1, ...), custom_call_target="tpu_custom_call" | custom-call | tf_op jit(solution)/shard_map/momentum/pallas_call | solution.py:62
  16.4 0.0 copy-start
  16.4 1.4 copy-done
  17.8 0.0 copy-start.1
  17.8 0.9 copy-done.1
  18.7 216.5 %exchange.1 = (bf16[16,384,256]{2,1,0:T(8,128)(2,1)}, bf16[16,384,128]{2,1,0:T(8,128)(2,1)S(1)}) custom-call(bf16[16,384,256]{2,1,0:T(8,128)(2,1)} %get-tuple-element.11.b1_ref, bf16[16,384,128]{2,1,0:T(8,128)(2,1)S(1)} %copy-done, f32[16,16,128]{2,1,0:T(8,128)S(1)} %copy-done.1), custom_call_target="tpu_custom_call" | custom-call | tf_op jit(solution)/shard_map/exchange/pallas_call | solution.py:241
  235.2 0.0 copy-start.2
  235.2 7.8 %multiply_subtract_fusion = f32[16,384,256]{2,1,0:T(8,128)} fusion(f32[16,384,256]{2,1,0:T(8,128)} %param.6, bf16[16,384,256]{2,1,0:T(8,128)(2,1)} %get-tuple-element.14), kind=kLoop, calls=%fused_computation | loop fusion | flops 9437184 | bytes 15728640 | tf_op jit(solution)/shard_map/sub | solution.py:262
  243.0 0.0 copy-done.2
  243.0 2.3 multiply_subtract_fusion.1
Async XLA Ops:
  16.4 1.4 copy-start
  17.8 0.9 copy-start.1
  235.2 7.8 %copy-start.2 = (f32[16,384,128]{2,1,0:T(8,128)S(1)}, f32[16,384,128]{2,1,0:T(8,128)}, u32[]{:S(2)}) copy-start(f32[16,384,128]{2,1,0:T(8,128)} %param.9) | copy-start | bytes 9437188

commit v2 on v0

v2 whole, which is shorter than its diff:
```python
import math
import jax
import jax.numpy as jnp
from jax import lax
from jax.experimental import pallas as pl
from jax.experimental.pallas import tpu as pltpu
from jax.sharding import PartitionSpec as P

NS_STEPS = 5
NS_COEF_A = 3.4445
NS_COEF_B = -4.7750
NS_COEF_C = 2.0315
MOMENTUM = 0.95
LEARN_RATE = 0.04
DECAY = 0.2
NORM_EPS = 1e-7

F32 = jnp.float32
BF16 = jnp.bfloat16
MESH = pl.DeviceIdType.MESH
TILE = 256
RETURN_STEP = 3
DZ_FAST = True
SWAP = True


def flip(bit, offset):
    return bit + offset - 2 * bit * offset


def xor2(value, offset):
    high = flip(lax.div(value, 2), lax.div(offset, 2))
    low = flip(lax.rem(value, 2), lax.rem(offset, 2))
    return high * 2 + low


def fold_squares(mom):
    sq = mom * mom
    rows, cols = sq.shape
    acc = jnp.sum(sq.reshape(rows // 8, 8, cols), axis=0)
    out = acc[:, :128]
    for col in range(128, cols, 128):
        out = out + acc[:, col:col + 128]
    return out


def dot_tn(lhs, rhs):
    return lax.dot_general(lhs, rhs, (((0,), (0,)), ((), ())), preferred_element_type=F32)


def gram_and_poly(x, gram, poly):
    size = gram.shape[0]
    for blk in range(size // TILE):
        lo, hi = blk * TILE, (blk + 1) * TILE
        val = dot_tn(x[:, lo:hi], x[:, :hi]).astype(BF16)
        gram[lo:hi, :hi] = val
        if blk:
            gram[:lo, lo:hi] = val[:, :lo].T
    for blk in range(size // TILE):
        lo, hi = blk * TILE, (blk + 1) * TILE
        sq = jnp.dot(gram[lo:hi, :], gram[:, :hi], preferred_element_type=F32)
        val = (NS_COEF_B * gram[lo:hi, :hi].astype(F32) + NS_COEF_C * sq).astype(BF16)
        poly[lo:hi, :hi] = val
        if blk:
            poly[:lo, lo:hi] = val[:, :lo].T


def update_rows(x, poly, rows):
    old = x[rows, :]
    term = jnp.dot(old, poly[...], preferred_element_type=F32)
    x[rows, :] = (NS_COEF_A * old.astype(F32) + term).astype(BF16)


def newton_schulz(x, gram, poly, block_rows, before_step, last_rows):
    blocks = x.shape[0] // block_rows

    def one_block(i, carry):
        update_rows(x, poly, pl.ds(pl.multiple_of(i * block_rows, block_rows), block_rows))
        return carry

    def one_step(step, carry):
        before_step(step)
        gram_and_poly(x, gram, poly)

        @pl.when(step < NS_STEPS - 1)
        def _():
            lax.fori_loop(0, blocks, one_block, 0)
        return carry
    lax.fori_loop(0, NS_STEPS, one_step, 0)
    last_rows()


def muon_kernel(w1_ref, m1_ref, g1_ref, w2_ref, m2_ref, g2_ref,
                nw1, nm1, nw2, nm2,
                b1, b2, x1, x2, o1, o2, gram1, poly1, gram2, poly2, sq_out, sq_in,
                m_load, g_load, w_load, in_send, in_recv, sq_send, sq_recv, out_send, out_recv):
    data = lax.axis_index('data')
    model = lax.axis_index('model')
    core = lax.rem(data, 2)
    me = data * 4 + model
    rows = b1.shape[1]
    stacks = ((m1_ref, g1_ref, w1_ref, nw1, nm1, b1, x1, o1, b1.shape[2]),
              (m2_ref, g2_ref, w2_ref, nw2, nm2, b2, x2, o2, b2.shape[2]))

    def peer(slot):
        return xor2(data, lax.rem(slot, 4)), xor2(model, lax.div(slot, 4))

    def expert_of(slot):
        to_data, to_model = peer(slot)
        return to_data * 4 + to_model

    def loop(lo, hi, action):
        def body(i, carry):
            action(i)
            return carry
        lax.fori_loop(lo, hi, body, 0)

    inner = flip(lax.rem(model, 2), lax.div(model, 2))

    def slot_of(dz, dd):
        high = lax.div(dz, 2)
        if SWAP:
            dz = high * 2 + flip(lax.rem(dz, 2), high * inner)
        return dz * 4 + dd

    def slot_at(i):
        if DZ_FAST:
            return slot_of(lax.rem(i, 4), lax.div(i, 4))
        return slot_of(lax.div(i, 4), lax.rem(i, 4))

    def core_slots(target_core, action):
        low = flip(core, target_core)

        def at(j):
            if DZ_FAST:
                return slot_of(lax.rem(j, 4), lax.div(j, 4) * 2 + low)
            return slot_of(lax.div(j, 2), lax.rem(j, 2) * 2 + low)
        loop(0, 8, lambda j: action(at(j)))

    def row_slice(index):
        return pl.ds(pl.multiple_of(index * rows, rows), rows)

    def col_slice(index, cols):
        return pl.ds(pl.multiple_of(index * cols, cols), cols)

    def remote(source, target, send, recv, slot):
        to_data, to_model = peer(slot)
        return pltpu.make_async_remote_copy(
            src_ref=source, dst_ref=target, send_sem=send, recv_sem=recv,
            device_id={'data': to_data, 'model': to_model}, device_id_type=MESH)

    def load_m(which, slot):
        e = expert_of(slot)
        return pltpu.make_async_copy(stacks[which][0].at[e], stacks[which][4].at[e], m_load.at[which, slot])

    def load_g(which, slot):
        e = expert_of(slot)
        return pltpu.make_async_copy(stacks[which][1].at[e], stacks[which][5].at[e], g_load.at[which, slot])

    def load_w(which):
        return pltpu.make_async_copy(stacks[which][2], stacks[which][3], w_load.at[which])

    def copy_sq(which, slot):
        return remote(sq_out.at[which, slot], sq_in.at[which, slot],
                      sq_send.at[which, slot], sq_recv.at[which, slot], slot)

    def copy_in(which, slot):
        src, dst, cols = stacks[which][5], stacks[which][6], stacks[which][8]
        return remote(src.at[expert_of(slot)], dst.at[row_slice(data), col_slice(model, cols)],
                      in_send.at[which, slot], in_recv.at[which, slot], slot)

    def copy_out(which, slot):
        src, dst, cols = stacks[which][6], stacks[which][7], stacks[which][8]
        to_data, to_model = peer(slot)
        return remote(src.at[row_slice(to_data), col_slice(to_model, cols)], dst.at[me],
                      out_send.at[which, slot], out_recv.at[which, slot], slot)

    def momentum(which, slot):
        nm, blocks = stacks[which][4], stacks[which][5]
        e = expert_of(slot)
        load_m(which, slot).wait()
        load_g(which, slot).wait()
        mom = MOMENTUM * nm[e] + blocks[e].astype(F32)
        nm[e] = mom
        blocks[e] = mom.astype(BF16)
        sq_out[which, slot] = fold_squares(mom)

    def norm_of(which):
        loop(1, 16, lambda slot: copy_sq(which, slot).wait_recv())
        total = jnp.sum(sq_in[which], axis=0)
        return jnp.sqrt(jnp.sum(total, keepdims=True)) + NORM_EPS

    def receive(which):
        blocks, x, cols = stacks[which][5], stacks[which][6], stacks[which][8]
        sq_in[which, 0] = sq_out[which, 0]
        norm = norm_of(which)
        own = (row_slice(data), col_slice(model, cols))
        x[own] = (blocks[me].astype(F32) / norm).astype(BF16)

        def take(slot):
            copy_in(which, slot).wait_recv()
            from_data, from_model = peer(slot)
            at = (row_slice(from_data), col_slice(from_model, cols))
            x[at] = (x[at].astype(F32) / norm).astype(BF16)
        loop(1, 16, take)

    def weight_step(which, e, ortho):
        new_w, x, cols = stacks[which][3], stacks[which][6], stacks[which][8]
        scale = 0.2 * math.sqrt(max(x.shape[0], x.shape[1]))
        old = new_w[e]
        new_w[e] = old - LEARN_RATE * (ortho.astype(F32) * scale + DECAY * old)

    def own_step(which):
        x, cols = stacks[which][6], stacks[which][8]
        weight_step(which, me, x[row_slice(data), col_slice(model, cols)])

    def peer_step(which, slot):
        copy_out(which, slot).wait_recv()
        e = expert_of(slot)
        weight_step(which, e, stacks[which][7][e])

    for which in (1, 0):
        def load(slot):
            load_m(which, slot).start()
            load_g(which, slot).start()
        if which:
            loop(1, 16, lambda i: load(slot_at(i)))
            load(0)
        else:
            loop(0, 16, load)
    load_w(1).start()
    load_w(0).start()

    barrier = pltpu.get_barrier_semaphore()

    def greet(slot):
        to_data, to_model = peer(slot)
        pl.semaphore_signal(barrier, inc=1, device_id={'data': to_data, 'model': to_model}, device_id_type=MESH)
    loop(1, 16, greet)
    pl.semaphore_wait(barrier, 15)

    def send2(slot):
        copy_sq(1, slot).start()
        copy_in(1, slot).start()

    def first(i):
        momentum(1, slot_at(i))

        @pl.when(i > 1)
        def _():
            send2(slot_at(i - 1))
    loop(1, 16, first)
    momentum(1, 0)
    send2(slot_at(15))

    loop(0, 16, lambda i: momentum(0, 15 - i))
    loop(1, 16, lambda slot: copy_sq(0, slot).start())

    def send1(slot):
        @pl.when(slot > 0)
        def _():
            copy_in(0, slot).start()
    core_slots(0, send1)
    core_slots(1, send1)

    receive(1)

    def finish2():
        loop(0, 4, lambda i: update_rows(x2, poly2, row_slice(i)))
    newton_schulz(x2, gram2, poly2, rows, lambda step: None, finish2)

    receive(0)
    return_step = (1 - core) * RETURN_STEP

    def before_step(step):
        @pl.when(step == return_step)
        def _():
            loop(1, 16, lambda i: copy_out(1, slot_at(i)).start())

    def finish1():
        update_rows(x1, poly1, row_slice(data))

        def body(dd):
            update_rows(x1, poly1, row_slice(xor2(data, dd)))
            for dz in range(4):
                slot = slot_of(dz, dd - 1)

                @pl.when(slot > 0)
                def _():
                    copy_out(0, slot).start()
        loop(1, 4, body)
        load_w(1).wait()
        own_step(1)
        for dz in range(4):
            copy_out(0, slot_of(dz, 3)).start()
    newton_schulz(x1, gram1, poly1, rows, before_step, finish1)

    load_w(0).wait()
    own_step(0)
    loop(1, 16, lambda slot: peer_step(1, slot))
    for which in (1, 0):
        def sent(slot):
            copy_in(which, slot).wait_send()
            copy_sq(which, slot).wait_send()
        loop(1, 16, sent)
    for target_core in (0, 1):
        def take(slot):
            @pl.when(slot > 0)
            def _():
                peer_step(0, slot)
        core_slots(target_core, take)
    for which in (1, 0):
        loop(1, 16, lambda slot: copy_out(which, slot).wait_send())


def solution(mesh):
    block_spec = P('stage', 'data', 'model')

    def local_step(w1, m1, g1, w2, m2, g2):
        experts, rows, cols1 = m1.shape
        cols2 = m2.shape[2]
        full_rows, size1, size2 = rows * 4, cols1 * 4, cols2 * 4
        dma = pltpu.SemaphoreType.DMA
        scratch = [pltpu.VMEM(g1.shape, BF16), pltpu.VMEM(g2.shape, BF16),
                   pltpu.VMEM((full_rows, size1), BF16), pltpu.VMEM((full_rows, size2), BF16),
                   pltpu.VMEM(g1.shape, BF16), pltpu.VMEM(g2.shape, BF16),
                   pltpu.VMEM((size1, size1), BF16), pltpu.VMEM((size1, size1), BF16),
                   pltpu.VMEM((size2, size2), BF16), pltpu.VMEM((size2, size2), BF16),
                   pltpu.VMEM((2, 16, 8, 128), F32), pltpu.VMEM((2, 16, 8, 128), F32),
                   dma((2, 16)), dma((2, 16)), dma((2,))] + [dma((2, 16))] * 6
        return pl.pallas_call(
            muon_kernel,
            out_shape=tuple(pltpu.VMEM(a.shape, F32) for a in (w1, m1, w2, m2)),
            in_specs=[pl.BlockSpec(memory_space=pl.ANY)] * 6,
            out_specs=(pl.BlockSpec(memory_space=pltpu.VMEM),) * 4,
            scratch_shapes=scratch,
            compiler_params=pltpu.CompilerParams(
                collective_id=0, has_side_effects=True, vmem_limit_bytes=36 << 20),
            name='muon')(w1, m1, g1, w2, m2, g2)

    return jax.shard_map(local_step, mesh=mesh, in_specs=(block_spec,) * 6, out_specs=(block_spec,) * 4, check_vma=False)
```

time: 744 us -> 227 us (0.31)
  matrix products: 365 us -> 0 us
  Pallas kernels: 0 us -> 217 us
  waiting for transfers between devices: 187 us -> 0 us
  blocking collectives: 106 us -> 0 us
  other arithmetic: 26.6 us -> 0 us
  local copies, waits for them, and re-layouts: 32.5 us -> 8.74 us
  between operations: 14.6 us -> 0.64 us
  starting transfers between devices: 8.54 us -> 0 us
    dot_general x26 -> x0, matrix products: 365 us -> none  [the longest x10 179 us: newton_schulz(): jnp.einsum('emk,ekn->emn', x_mat, poly_mat, preferred_element_type=jnp.fl...]
    pallas_call x0 -> x1, Pallas kernels: none -> 217 us  [local_step(): pl.pallas_call(muon_kernel, out_shape=tuple((pltpu.VMEM(a.shape, F32) for...]
    all_gather x2 -> x0, waiting for transfers between devices: 155 us -> none  [update_stack(): mom_whole = lax.all_gather(row_whole, 'model', axis=2, tiled=True)]
    all_to_all x2 -> x0, blocking collectives: 63.6 us -> none  [update_stack(): lax.all_to_all(new_mom.astype(jnp.bfloat16), 'data', 0, 1, tiled=True)]
    psum x1 -> x0, blocking collectives: 42.8 us -> none  [update_stack(): lax.psum(jnp.sum(new_mom * new_mom, axis=(1, 2)), ('data', 'model'))]
    all_to_all x2 -> x0, waiting for transfers between devices: 31.9 us -> none  [update_stack(): x_back = lax.all_to_all(x_cols, 'data', 1, 0, tiled=True)]
    dynamic_slice x2 -> x0, local copies, waits for them, and re-layouts: 21.5 us -> none  [update_stack(): lax.dynamic_slice_in_dim(x_mat, lax.axis_index('model') * cols_loc, cols_...]
    convert_element_type x4 -> x0, other arithmetic: 10.7 us -> none  [the longest x2 7.37 us: newton_schulz(): (NS_COEF_A * x_mat.astype(jnp.float32) + update_term).astype(jnp.bfloat16)]
  transfers between devices with their start and end apart: 4 -> 0, of which waited for: 3 -> 0; matrix products, arithmetic and copies ran while one was open for 55% -> 0% of each run, Pallas kernels for 0% -> 0%
where the time goes in v2:
time: 227 us; the launch traced here: 226 us
  Pallas kernels  217 us (96%)
  local copies, waits for them, and re-layouts  8.74 us (4%)
    pallas_call x1, Pallas kernels, local_step(): pl.pallas_call(muon_kernel, out_shape=tuple((pltpu.VMEM(a.shape, F32) for...  217 us
    unnamed x4, local copies, waits for them, and re-layouts  8.74 us

profile of v2, /device:TPU:0, one launch (start us, length us, event | category | flops | bytes accessed | tf_op | source)
XLA Modules:
  0.0 226.1 jit_solution(4646047325617108929)
XLA Ops:
  0.6 216.8 %muon.1 = (f32[16,384,256]{2,1,0:T(8,128)S(1)}, f32[16,384,256]{2,1,0:T(8,128)S(1)}, f32[16,384,128]{2,1,0:T(8,128)S(1)}, f32[16,384,128]{2,1,0:T(8,128)S(1)}) custom-call(f32[16,384,256]{2,1,0:T(8,128)} %w1_ref.1, f32[16,384,256]{2,1,0:T(8,128)} %m1_ref.1, bf16[16,384,256]{2,1,0:T(8,128)(2,1)} %g1_ref.1, f32[16,384,128]{2,1,0:T(8,128)} %w2_ref.1, ...), custom_call_target="tpu_custom_call" | custom-call | tf_op jit(solution)/shard_map/muon/pallas_call | solution.py:331
  217.4 2.7 %copy.14 = f32[16,384,256]{2,1,0:T(8,128)} copy(f32[16,384,256]{2,1,0:T(8,128)S(1)} %get-tuple-element.4) | data formatting | bytes 12582912
  220.1 1.7 copy.16
  221.8 1.7 copy.17
  223.4 2.7 %copy.15 = f32[16,384,256]{2,1,0:T(8,128)} copy(f32[16,384,256]{2,1,0:T(8,128)S(1)} %get-tuple-element.5) | data formatting | bytes 12582912

commit v3 on v2

--- a/solution.py
+++ b/solution.py
@@ -19,7 +19,6 @@
 BF16 = jnp.bfloat16
 MESH = pl.DeviceIdType.MESH
 TILE = 256
-RETURN_STEP = 3
 DZ_FAST = True
 SWAP = True
 
@@ -71,7 +70,7 @@
     x[rows, :] = (NS_COEF_A * old.astype(F32) + term).astype(BF16)
 
 
-def newton_schulz(x, gram, poly, block_rows, before_step, last_rows):
+def newton_schulz(x, gram, poly, block_rows, last_rows):
     blocks = x.shape[0] // block_rows
 
     def one_block(i, carry):
@@ -79,7 +78,6 @@
         return carry
 
     def one_step(step, carry):
-        before_step(step)
         gram_and_poly(x, gram, poly)
 
         @pl.when(step < NS_STEPS - 1)
@@ -133,7 +131,7 @@
 
         def at(j):
             if DZ_FAST:
-                return slot_of(lax.rem(j, 4), lax.div(j, 4) * 2 + low)
+                return slot_of(lax.rem(j + 2 * core, 4), lax.div(j, 4) * 2 + low)
             return slot_of(lax.div(j, 2), lax.rem(j, 2) * 2 + low)
         loop(0, 8, lambda j: action(at(j)))
 
@@ -267,23 +265,17 @@
 
     def finish2():
         loop(0, 4, lambda i: update_rows(x2, poly2, row_slice(i)))
-    newton_schulz(x2, gram2, poly2, rows, lambda step: None, finish2)
+    newton_schulz(x2, gram2, poly2, rows, finish2)
+    loop(1, 16, lambda i: copy_out(1, slot_at(i)).start())
 
     receive(0)
-    return_step = (1 - core) * RETURN_STEP
-
-    def before_step(step):
-        @pl.when(step == return_step)
-        def _():
-            loop(1, 16, lambda i: copy_out(1, slot_at(i)).start())
-
     def finish1():
         update_rows(x1, poly1, row_slice(data))
 
         def body(dd):
             update_rows(x1, poly1, row_slice(xor2(data, dd)))
             for dz in range(4):
-                slot = slot_of(dz, dd - 1)
+                slot = slot_of(lax.rem(dz + 2 * core, 4), dd - 1)
 
                 @pl.when(slot > 0)
                 def _():
@@ -292,8 +284,8 @@
         load_w(1).wait()
         own_step(1)
         for dz in range(4):
-            copy_out(0, slot_of(dz, 3)).start()
-    newton_schulz(x1, gram1, poly1, rows, before_step, finish1)
+            copy_out(0, slot_of(lax.rem(dz + 2 * core, 4), 3)).start()
+    newton_schulz(x1, gram1, poly1, rows, finish1)
 
     load_w(0).wait()
     own_step(0)
@@ -313,6 +305,32 @@
         loop(1, 16, lambda slot: copy_out(which, slot).wait_send())
 
 
+def store_kernel(*refs):
+    sources, targets, sems = refs[:4], refs[4:8], refs[8]
+    step = 4
+    copies = []
+    for which in range(4):
+        for part in range(16 // step):
+            at = pl.ds(part * step, step)
+            copies.append(pltpu.make_async_copy(
+                sources[which].at[at], targets[which].at[at], sems.at[which, part]))
+    for copy in copies:
+        copy.start()
+    for copy in copies:
+        copy.wait()
+
+
+def store(arrays):
+    return pl.pallas_call(
+        store_kernel,
+        out_shape=tuple(jax.ShapeDtypeStruct(a.shape, a.dtype) for a in arrays),
+        in_specs=[pl.BlockSpec(memory_space=pltpu.VMEM)] * 4,
+        out_specs=(pl.BlockSpec(memory_space=pl.ANY),) * 4,
+        scratch_shapes=[pltpu.SemaphoreType.DMA((4, 4))],
+        compiler_params=pltpu.CompilerParams(vmem_limit_bytes=1 << 20),
+        name='store')(*(pltpu.with_memory_space_constraint(a, pltpu.VMEM) for a in arrays))
+
+
 def solution(mesh):
     block_spec = P('stage', 'data', 'model')
 
@@ -328,7 +346,7 @@
                    pltpu.VMEM((size2, size2), BF16), pltpu.VMEM((size2, size2), BF16),
                    pltpu.VMEM((2, 16, 8, 128), F32), pltpu.VMEM((2, 16, 8, 128), F32),
                    dma((2, 16)), dma((2, 16)), dma((2,))] + [dma((2, 16))] * 6
-        return pl.pallas_call(
+        return store(pl.pallas_call(
             muon_kernel,
             out_shape=tuple(pltpu.VMEM(a.shape, F32) for a in (w1, m1, w2, m2)),
             in_specs=[pl.BlockSpec(memory_space=pl.ANY)] * 6,
@@ -336,6 +354,6 @@
             scratch_shapes=scratch,
             compiler_params=pltpu.CompilerParams(
                 collective_id=0, has_side_effects=True, vmem_limit_bytes=36 << 20),
-            name='muon')(w1, m1, g1, w2, m2, g2)
+            name='muon')(w1, m1, g1, w2, m2, g2))
 
     return jax.shard_map(local_step, mesh=mesh, in_specs=(block_spec,) * 6, out_specs=(block_spec,) * 4, check_vma=False)

time: 227 us -> 225 us (level)
  local copies, waits for them, and re-layouts: 8.74 us -> 0 us
  Pallas kernels: 217 us -> 224 us
    unnamed x4 -> x0, local copies, waits for them, and re-layouts: 8.74 us -> none
    pallas_call x0 -> x1, Pallas kernels: none -> 6.6 us  [store(): pl.pallas_call(store_kernel, out_shape=tuple((jax.ShapeDtypeStruct(a.shap...]
where the time goes in v3:
time: 225 us
  Pallas kernels  224 us (100%)
    pallas_call x1, Pallas kernels, local_step(): pl.pallas_call(muon_kernel, out_shape=tuple((pltpu.VMEM(a.shape, F32) for...  217 us
    pallas_call x1, Pallas kernels, store(): pl.pallas_call(store_kernel, out_shape=tuple((jax.ShapeDtypeStruct(a.shap...  6.6 us

profile of v3, /device:TPU:0, one launch (start us, length us, event | category | flops | bytes accessed | tf_op | source)
XLA Modules:
  0.0 224.5 jit_solution(15359418614587499633)
XLA Ops:
  0.6 217.3 %muon.1 = (f32[16,384,256]{2,1,0:T(8,128)S(1)}, f32[16,384,256]{2,1,0:T(8,128)S(1)}, f32[16,384,128]{2,1,0:T(8,128)S(1)}, f32[16,384,128]{2,1,0:T(8,128)S(1)}) custom-call(f32[16,384,256]{2,1,0:T(8,128)} %w1_ref.1, f32[16,384,256]{2,1,0:T(8,128)} %m1_ref.1, bf16[16,384,256]{2,1,0:T(8,128)(2,1)} %g1_ref.1, f32[16,384,128]{2,1,0:T(8,128)} %w2_ref.1, ...), custom_call_target="tpu_custom_call" | custom-call | tf_op jit(solution)/shard_map/muon/pallas_call | solution.py:349
  217.9 6.6 %store.1 = (f32[16,384,256]{2,1,0:T(8,128)}, f32[16,384,256]{2,1,0:T(8,128)}, f32[16,384,128]{2,1,0:T(8,128)}, f32[16,384,128]{2,1,0:T(8,128)}) custom-call(f32[16,384,256]{2,1,0:T(8,128)S(1)} %get-tuple-element.8.refs_0_, f32[16,384,256]{2,1,0:T(8,128)S(1)} %get-tuple-element.9.refs_1_, f32[16,384,128]{2,1,0:T(8,128)S(1)} %get-tuple-element.10.refs_2_, ...), custom_call_target="tpu_custom_call" | custom-call | tf_op jit(solution)/shard_map/store/pallas_call | solution.py:324

commit v4 on v3

--- a/solution.py
+++ b/solution.py
@@ -270,21 +270,23 @@
 
     receive(0)
     def finish1():
-        update_rows(x1, poly1, row_slice(data))
-
-        def body(dd):
-            update_rows(x1, poly1, row_slice(xor2(data, dd)))
+        update_rows(x1, poly1, row_slice(xor2(data, 3)))
+
+        def send_rows(dd):
             for dz in range(4):
-                slot = slot_of(lax.rem(dz + 2 * core, 4), dd - 1)
+                slot = slot_of(lax.rem(dz + 2 * core, 4), dd)
 
                 @pl.when(slot > 0)
                 def _():
                     copy_out(0, slot).start()
+
+        def body(i):
+            update_rows(x1, poly1, row_slice(xor2(data, 3 - i)))
+            send_rows(4 - i)
         loop(1, 4, body)
         load_w(1).wait()
         own_step(1)
-        for dz in range(4):
-            copy_out(0, slot_of(lax.rem(dz + 2 * core, 4), 3)).start()
+        send_rows(0)
     newton_schulz(x1, gram1, poly1, rows, finish1)
 
     load_w(0).wait()
@@ -307,7 +309,7 @@
 
 def store_kernel(*refs):
     sources, targets, sems = refs[:4], refs[4:8], refs[8]
-    step = 4
+    step = 2
     copies = []
     for which in range(4):
         for part in range(16 // step):
@@ -326,7 +328,7 @@
         out_shape=tuple(jax.ShapeDtypeStruct(a.shape, a.dtype) for a in arrays),
         in_specs=[pl.BlockSpec(memory_space=pltpu.VMEM)] * 4,
         out_specs=(pl.BlockSpec(memory_space=pl.ANY),) * 4,
-        scratch_shapes=[pltpu.SemaphoreType.DMA((4, 4))],
+        scratch_shapes=[pltpu.SemaphoreType.DMA((4, 8))],
         compiler_params=pltpu.CompilerParams(vmem_limit_bytes=1 << 20),
         name='store')(*(pltpu.with_memory_space_constraint(a, pltpu.VMEM) for a in arrays))
 

time: 225 us -> 226 us (level); the launches traced: 225 us -> 221 us
  Pallas kernels: 224 us -> 221 us
    pallas_call x1, Pallas kernels: 217 us -> 214 us  [local_step(): pl.pallas_call(muon_kernel, out_shape=tuple((pltpu.VMEM(a.shape, F32) for...]
where the time goes in v4:
time: 226 us; the launch traced here: 221 us
  Pallas kernels  221 us (98%)
    pallas_call x1, Pallas kernels, local_step(): pl.pallas_call(muon_kernel, out_shape=tuple((pltpu.VMEM(a.shape, F32) for...  214 us
    pallas_call x1, Pallas kernels, store(): pl.pallas_call(store_kernel, out_shape=tuple((jax.ShapeDtypeStruct(a.shap...  6.72 us

profile of v4, /device:TPU:0, one launch (start us, length us, event | category | flops | bytes accessed | tf_op | source)
XLA Modules:
  0.0 221.2 jit_solution(15759999271895827812)
XLA Ops:
  0.6 213.8 %muon.1 = (f32[16,384,256]{2,1,0:T(8,128)S(1)}, f32[16,384,256]{2,1,0:T(8,128)S(1)}, f32[16,384,128]{2,1,0:T(8,128)S(1)}, f32[16,384,128]{2,1,0:T(8,128)S(1)}) custom-call(f32[16,384,256]{2,1,0:T(8,128)} %w1_ref.1, f32[16,384,256]{2,1,0:T(8,128)} %m1_ref.1, bf16[16,384,256]{2,1,0:T(8,128)(2,1)} %g1_ref.1, f32[16,384,128]{2,1,0:T(8,128)} %w2_ref.1, ...), custom_call_target="tpu_custom_call" | custom-call | tf_op jit(solution)/shard_map/muon/pallas_call | solution.py:351
  214.5 6.7 %store.1 = (f32[16,384,256]{2,1,0:T(8,128)}, f32[16,384,256]{2,1,0:T(8,128)}, f32[16,384,128]{2,1,0:T(8,128)}, f32[16,384,128]{2,1,0:T(8,128)}) custom-call(f32[16,384,256]{2,1,0:T(8,128)S(1)} %get-tuple-element.8.refs_0_, f32[16,384,256]{2,1,0:T(8,128)S(1)} %get-tuple-element.9.refs_1_, f32[16,384,128]{2,1,0:T(8,128)S(1)} %get-tuple-element.10.refs_2_, ...), custom_call_target="tpu_custom_call" | custom-call | tf_op jit(solution)/shard_map/store/pallas_call | solution.py:326
